TPU v7x, 32 devices: a whole 2x2x4 slice. The times are simulated.
32 devices in a mesh: dp: 2 (over x), tp: 16 (over y, z, core).
Axes of the slice: x: 2, y: 2, z: 4, core: 2. Of those that a mesh axis runs over, the one named last changes fastest.
Arguments:
- x: bfloat16 [8192, 4096], P(('dp', 'tp')), parts along dimension 0
- w_gate: bfloat16 [4096, 12288], P(None, 'tp')
- w_up: bfloat16 [4096, 12288], P(None, 'tp')
- w_down: bfloat16 [12288, 4096], P('tp')
Outputs:
- output: bfloat16 [8192, 4096], P(('dp', 'tp')), parts along dimension 0
There are 2 independent parts. A program takes and returns all parts, laid end to end along the dimension named above; an argument that names none is the same for every part.
All inputs are finite; a program needn't handle non-finite values.
Results may differ from a plain program's by a relative error of at most 0.016.
Values are sent between devices in bfloat16 or wider.
A program may use at most 2 GiB of HBM per device.

v0:
```python
import jax
import jax.numpy as jnp
from jax import lax
from jax.sharding import PartitionSpec as P


def solution(mesh):
    def step(x, w_gate, w_up, w_down):
        rows = lax.all_gather(x, "tp", axis=0, tiled=True)
        gate = jnp.dot(rows, w_gate, preferred_element_type=jnp.float32)
        up = jnp.dot(rows, w_up, preferred_element_type=jnp.float32)
        hidden = (jax.nn.silu(gate) * up).astype(jnp.bfloat16)
        term = jnp.dot(hidden, w_down, preferred_element_type=jnp.float32).astype(jnp.bfloat16)
        return lax.psum_scatter(term, "tp", scatter_dimension=0, tiled=True)

    return jax.shard_map(
        step,
        mesh=mesh,
        in_specs=(P(("dp", "tp"), None), P(None, "tp"), P(None, "tp"), P("tp", None)),
        out_specs=P(("dp", "tp"), None),
        check_vma=False,
    )
```

profile of v0, /device:TPU:0, one launch (start us, length us, event | category | flops | bytes accessed | tf_op | source)
XLA Modules:
  0.0 614.7 jit_solution(8345221276371351631)
XLA Ops:
  6.5 0.0 all-gather.2.cloned.1.call-start
  6.5 0.7 all-gather.2.cloned.1.call-update
  7.3 0.0 reduce-scatter.2.cloned.1.call-start
  7.3 172.3 %all-gather.2.cloned.1.call-done = bf16[4096,4096]{1,0:T(8,128)(2,1)} async-done(((bf16[256,4096]{1,0:T(8,128)(2,1)}), bf16[4096,4096]{1,0:T(8,128)(2,1)}) %all-gather.2.cloned.1.call-update) | async-done | bytes 33554448 | tf_op jit(solution)/shard_map/all_gather | solution.py:9
  179.7 31.8 %fusion.1 = f32[4096,768]{1,0:T(8,128)S(1)} fusion(bf16[4096,4096]{1,0:T(8,128)(2,1)} %all-gather.2.cloned.1.call-done, bf16[4096,768]{1,0:T(8,128)(2,1)} %param.5), kind=kOutput, calls=%fused_computation.3 | convolution fusion | flops 25769803776 | bytes 52428800 | tf_op jit(solution)/shard_map/dot_general | solution.py:10
  211.4 33.9 %multiply_convert_fusion.clone.4 = bf16[4096,768]{1,0:T(8,128)(2,1)} fusion(f32[4096,768]{1,0:T(8,128)S(1)} %fusion.1, bf16[4096,4096]{1,0:T(8,128)(2,1)} %all-gather.2.cloned.1.call-done, bf16[4096,768]{1,0:T(8,128)(2,1)} %param.6), kind=kOutput, calls=%fused_computation.1.clone.clone.clone.1 | convolution fusion | flops 25788678144 | bytes 58720256 | tf_op jit(solution)/shard_map/dot_general | solution.py:11
  245.3 34.2 %convolution_convert_fusion = bf16[4096,4096]{1,0:T(8,128)(2,1)} fusion(bf16[768,4096]{1,0:T(8,128)(2,1)} %param.7, bf16[4096,768]{1,0:T(8,128)(2,1)} %multiply_convert_fusion.clone.4), kind=kOutput, calls=%fused_computation | convolution fusion | flops 25786580992 | bytes 46137344 | tf_op jit(solution)/shard_map/dot_general | solution.py:13
  279.5 0.0 reduce-scatter.2.cloned.1.call-update
  279.6 328.3 %reduce-scatter.2.cloned.1.call-done = bf16[256,4096]{1,0:T(8,128)(2,1)} async-done(((bf16[4096,4096]{1,0:T(8,128)(2,1)}), bf16[256,4096]{1,0:T(8,128)(2,1)}) %reduce-scatter.2.cloned.1.call-update) | async-done | bytes 2097168 | tf_op jit(solution)/shard_map/reduce_scatter | solution.py:14
Async XLA Ops:
  6.5 173.1 %all-gather.2.cloned.1.call-start = ((), (), s32[]{:S(2)}) async-start(), calls=%async_computation.1 | async-start | bytes 35651584 | tf_op jit(solution)/shard_map/all_gather | solution.py:9
  7.3 600.6 %reduce-scatter.2.cloned.1.call-start = ((), (), s32[]{:S(2)}) async-start(), calls=%async_computation.2 | async-start | bytes 35651584 | tf_op jit(solution)/shard_map/reduce_scatter | solution.py:14
Sparse Core Ops, SparseCore 0:
  8.9 170.6 all-gather.1
  279.7 328.1 reduce-scatter.1
where the time goes:
time: 615 us
  waiting for transfers between devices  501 us (81%)
  matrix products  99.9 us (16%)
  between operations  13.4 us (2%)
    reduce_scatter x1, waiting for transfers between devices, step(): return lax.psum_scatter(term, 'tp', scatter_dimension=0, tiled=True)  328 us
    all_gather x1, waiting for transfers between devices, step(): rows = lax.all_gather(x, 'tp', axis=0, tiled=True)  172 us
    dot_general x1, matrix products, step(): jnp.dot(hidden, w_down, preferred_element_type=jnp.float32)  34.2 us
    dot_general x1, matrix products, step(): up = jnp.dot(rows, w_up, preferred_element_type=jnp.float32)  33.9 us
    dot_general x1, matrix products, step(): gate = jnp.dot(rows, w_gate, preferred_element_type=jnp.float32)  31.8 us
  transfers between devices with their start and end apart: 2, of which 2 were waited for; matrix products, arithmetic and copies ran while one was open for 0% of the time, Pallas kernels for 0%

commit v1 on v0

v1 whole, which is shorter than its diff:
```python
import functools

import jax
import jax.numpy as jnp
from jax import lax
from jax.experimental import pallas as pl
from jax.experimental.pallas import tpu as pltpu
from jax.sharding import PartitionSpec as P

CHIPS = 8
SLOTS = 4
MESH = pl.DeviceIdType.MESH


def chip_at(place):
    return jnp.where(place < 4, place, 11 - place)


def kernel(x_ref, wg_ref, wu_ref, wd_ref, out_ref, sum_ref,
           wg, wu, wd, xb, acc, own, hid, term, stage, other, got,
           w_sem, own_sem, load_sem, out_sem,
           x_send, x_recv, d_send, d_recv, t_send, t_recv, s_send, s_recv):
    rows = xb.shape[2] // 2
    depth, cols = wg.shape
    wide = wd.shape[1]
    tile = 512
    last = CHIPS - 1

    dp = lax.axis_index("dp")
    tp = lax.axis_index("tp")
    core = lax.rem(tp, 2)
    chip = tp // 2
    place = jnp.where(chip < 4, chip, 11 - chip)
    right = (dp, chip_at(lax.rem(place + 1, CHIPS)) * 2 + core)
    left = (dp, chip_at(lax.rem(place + CHIPS - 1, CHIPS)) * 2 + core)
    mate = (dp, tp + 1 - 2 * core)
    onward = (right, left)

    loads = [
        pltpu.make_async_copy(src, dst, w_sem.at[n])
        for n, (src, dst) in enumerate(((wg_ref, wg), (wu_ref, wu), (wd_ref, wd)))
    ]
    mine = [
        pltpu.make_async_copy(
            x_ref.at[pl.ds(d * rows, rows)], xb.at[d, 0, pl.ds(0, rows)], own_sem.at[d]
        )
        for d in range(2)
    ]
    for copy in mine + loads:
        copy.start()

    barrier = pltpu.get_barrier_semaphore()
    for peer in (left, right, mate):
        pl.semaphore_signal(barrier, inc=1, device_id=peer, device_id_type=MESH)
    pl.semaphore_wait(barrier, 3)

    def remote(src, dst, send, recv, peer):
        return pltpu.make_async_remote_copy(
            src_ref=src, dst_ref=dst, send_sem=send, recv_sem=recv,
            device_id=peer, device_id_type=MESH,
        )

    def pass_on(d, k, src=None):
        if src is None:
            src = xb.at[d, lax.rem(k, SLOTS), pl.ds(0, rows)]
        return remote(
            src, xb.at[d, lax.rem(k + 1, SLOTS), pl.ds(0, rows)],
            x_send.at[d, k], x_recv.at[d, k + 1], onward[d],
        )

    def share(d, k, src=None):
        slot = lax.rem(k, SLOTS)
        if src is None:
            src = xb.at[d, slot, pl.ds(0, rows)]
        return remote(
            src, xb.at[d, slot, pl.ds(rows, rows)], d_send.at[d, k], d_recv.at[d, k], mate
        )

    def give(d, k):
        return remote(
            term.at[d], other.at[d, lax.rem(k, 2)], t_send.at[d, k], t_recv.at[d, k], mate
        )

    def advance(d, k):
        return remote(
            stage.at[d, lax.rem(k, 2)], sum_ref.at[d, k + 1],
            s_send.at[d, k], s_recv.at[d, k + 1], onward[d],
        )

    def fetch(d, k):
        return pltpu.make_async_copy(sum_ref.at[d, k], got.at[d], load_sem.at[d])

    for d in range(2):
        pass_on(d, 0, x_ref.at[pl.ds(d * rows, rows)]).start()
    for d in range(2):
        share(d, 0, x_ref.at[pl.ds(d * rows, rows)]).start()
    for copy in mine + loads:
        copy.wait()

    def terms(d, k):
        slot = lax.rem(k, SLOTS)
        share(d, k).wait_recv()
        for n in range(cols // 256):
            part = pl.ds(n * 256, 256)
            gate = jnp.dot(xb[d, slot], wg[:, part], preferred_element_type=jnp.float32)
            up = jnp.dot(xb[d, slot], wu[:, part], preferred_element_type=jnp.float32)
            hid[:, part] = (jax.nn.silu(gate) * up).astype(hid.dtype)

        @pl.when(k > 0)
        def _():
            give(d, k - 1).wait_send()

        for n in range(wide // tile):
            part = pl.ds(n * tile, tile)
            both = jnp.dot(hid[...], wd[:, part], preferred_element_type=jnp.float32)
            acc[d, :, part] = both[:rows]
            term[d, :, part] = both[rows:].astype(term.dtype)
        give(d, k).start()

    def add(d, k):
        give(d, k).wait_recv()

        @pl.when(k >= 2)
        def _():
            fetch(d, k).wait()
            for n in range(wide // tile):
                part = pl.ds(n * tile, tile)
                acc[d, :, part] += got[d, :, part].astype(jnp.float32)

        slot = lax.rem(k, 2)

        @pl.when(k == 0)
        def _():
            for n in range(wide // tile):
                part = pl.ds(n * tile, tile)
                own[d, :, part] = acc[d, :, part] + other[d, slot, :, part].astype(jnp.float32)

        @pl.when(k >= 3)
        def _():
            advance(d, k - 2).wait_send()

        @pl.when(k >= 1)
        def _():
            for n in range(wide // tile):
                part = pl.ds(n * tile, tile)
                stage[d, slot, :, part] = (
                    acc[d, :, part] + other[d, slot, :, part].astype(jnp.float32)
                ).astype(stage.dtype)
            advance(d, k).start()

    @pl.loop(0, CHIPS)
    def _(k):
        @pl.when(k >= 1)
        def _():
            for d in range(2):
                pass_on(d, k - 1).wait_recv()

                @pl.when(k < last)
                def _():
                    pass_on(d, k).start()

                share(d, k).start()

        for d in range(2):
            terms(d, k)

        @pl.when(k >= 1)
        def _():
            for d in range(2):
                pass_on(d, k - 1).wait_send()
                share(d, k - 1).wait_send()

        @pl.when(k >= 2)
        def _():
            for d in range(2):
                advance(d, k - 1).wait_recv()
                fetch(d, k).start()

        for d in range(2):
            add(d, k)

    for d in range(2):
        advance(d, last).wait_recv()
        fetch(d, CHIPS).start()
    results = []
    for d in range(2):
        fetch(d, CHIPS).wait()
        advance(d, last - 1).wait_send()
        for n in range(wide // tile):
            part = pl.ds(n * tile, tile)
            stage[d, (last - 1) % 2, :, part] = (
                own[d, :, part] + got[d, :, part].astype(jnp.float32)
            ).astype(stage.dtype)
        copy = pltpu.make_async_copy(
            stage.at[d, (last - 1) % 2], out_ref.at[pl.ds(d * rows, rows)], out_sem.at[d]
        )
        copy.start()
        results.append(copy)
    for d in range(2):
        share(d, last).wait_send()
        give(d, last).wait_send()
        advance(d, last).wait_send()
        results[d].wait()


def solution(mesh):
    def step(x, w_gate, w_up, w_down):
        total, depth = x.shape
        rows = total // 2
        cols = w_gate.shape[1]
        wide = w_down.shape[1]
        dma = pltpu.SemaphoreType.DMA
        hops = (2, CHIPS + 1)
        b16, f32 = jnp.bfloat16, jnp.float32
        anywhere = pl.BlockSpec(memory_space=pl.ANY)
        out, _ = pl.pallas_call(
            kernel,
            name="ring",
            out_shape=(
                jax.ShapeDtypeStruct((total, wide), b16),
                jax.ShapeDtypeStruct((2, CHIPS + 1, rows, wide), b16),
            ),
            in_specs=[anywhere] * 4,
            out_specs=(anywhere, anywhere),
            scratch_shapes=[
                pltpu.VMEM((depth, cols), b16),
                pltpu.VMEM((depth, cols), b16),
                pltpu.VMEM((cols, wide), b16),
                pltpu.VMEM((2, SLOTS, 2 * rows, depth), b16),
                pltpu.VMEM((2, rows, wide), f32),
                pltpu.VMEM((2, rows, wide), f32),
                pltpu.VMEM((2 * rows, cols), b16),
                pltpu.VMEM((2, rows, wide), b16),
                pltpu.VMEM((2, 2, rows, wide), b16),
                pltpu.VMEM((2, 2, rows, wide), b16),
                pltpu.VMEM((2, rows, wide), b16),
                dma((3,)), dma((2,)), dma((2,)), dma((2,)),
                dma(hops), dma(hops), dma(hops), dma(hops),
                dma(hops), dma(hops), dma(hops), dma(hops),
            ],
            compiler_params=pltpu.CompilerParams(
                collective_id=0, has_side_effects=True, vmem_limit_bytes=67043328
            ),
            cost_estimate=pl.CostEstimate(
                flops=2 * 16 * total * depth * cols * 3,
                bytes_accessed=3 * depth * cols * 2 + 64 * total * depth * 2,
                transcendentals=16 * total * cols,
            ),
        )(x, w_gate, w_up, w_down)
        return out

    return jax.shard_map(
        step,
        mesh=mesh,
        in_specs=(P(("dp", "tp"), None), P(None, "tp"), P(None, "tp"), P("tp", None)),
        out_specs=P(("dp", "tp"), None),
        check_vma=False,
    )
```

time: 615 us -> 331 us (0.54)
  waiting for transfers between devices: 501 us -> 0 us
  Pallas kernels: 0 us -> 328 us
  matrix products: 99.9 us -> 0 us
  between operations: 13.4 us -> 0.01 us
    reduce_scatter x1 -> x0, waiting for transfers between devices: 328 us -> none  [step(): return lax.psum_scatter(term, 'tp', scatter_dimension=0, tiled=True)]
    pallas_call x0 -> x1, Pallas kernels: none -> 328 us  [step(): pl.pallas_call(kernel, name='ring', out_shape=(jax.ShapeDtypeStruct((tota...]
    all_gather x1 -> x0, waiting for transfers between devices: 172 us -> none  [step(): rows = lax.all_gather(x, 'tp', axis=0, tiled=True)]
    dot_general x3 -> x0, matrix products: 99.9 us -> none  [the longest x1 34.2 us: step(): jnp.dot(hidden, w_down, preferred_element_type=jnp.float32)]
  transfers between devices with their start and end apart: 2 -> 0, of which waited for: 2 -> 0; matrix products, arithmetic and copies ran while one was open for 0% -> 0% of each run, Pallas kernels for 0% -> 0%
where the time goes in v1:
time: 331 us
  Pallas kernels  328 us (99%)
    pallas_call x1, Pallas kernels, step(): pl.pallas_call(kernel, name='ring', out_shape=(jax.ShapeDtypeStruct((tota...  328 us

profile of v1, /device:TPU:0, one launch (start us, length us, event | category | flops | bytes accessed | tf_op | source)
XLA Modules:
  0.0 330.7 jit_solution(16957237096962640454)
XLA Ops:
  0.0 327.6 %ring.1 = (bf16[256,4096]{1,0:T(8,128)(2,1)}, bf16[2,9,128,4096]{3,2,1,0:T(8,128)(2,1)}) custom-call(bf16[256,4096]{1,0:T(8,128)(2,1)} %x_ref.1, bf16[4096,768]{1,0:T(8,128)(2,1)} %wg_ref.1, bf16[4096,768]{1,0:T(8,128)(2,1)} %wu_ref.1, bf16[768,4096]{1,0:T(8,128)(2,1)} %wd_ref.1), custom_call_target="tpu_custom_call" | custom-call | flops 77309411328 | bytes 153092096 | tf_op jit(solution)/shard_map/ring/pallas_call | solution.py:216
  327.6 3.1 copy.6

commit v2 on v0

v2 whole, which is shorter than its diff:
```python
import functools

import jax
import jax.numpy as jnp
from jax import lax
from jax.experimental import pallas as pl
from jax.experimental.pallas import tpu as pltpu
from jax.sharding import PartitionSpec as P

PARTS = 4
STAGES = 8
MESH = pl.DeviceIdType.MESH
PASS = (
    (
        5, 28, 13, 20, 57, 140, 49, 33, 89, 169, 160, 97,
        209, 216, 193, 224, 184, 233, 80, 40, 144, 64, 176, 152,
        104, 241, 248, 200, 112, 120, 72, 128,
    ),
    (
        62, 51, 45, 39, 91, 5, 180, 65, 170, 160, 98, 140,
        17, 29, 211, 194, 150, 234, 158, 80, 220, 132, 75, 243,
        12, 250, 224, 202, 184, 122, 104, 112,
    ),
)
PASS_END = (
    (
        9, 11, 11, 13, 16, 16, 16, 16, 21, 21, 22, 23,
        26, 26, 26, 26, 27, 29, 29, 30, 30, 31, 32, 32,
        32, 32, 32, 32, 32, 32, 32, 32,
    ),
    (
        12, 16, 19, 24, 24, 25, 26, 27, 27, 29, 29, 29,
        29, 29, 29, 31, 31, 31, 31, 31, 32, 32, 32, 32,
        32, 32, 32, 32, 32, 32, 32, 32,
    ),
)
WORK = (
    (
        131, 355, 643, 387, 867, 675, 833, 899, 769, 929, 579, 327,
        737, 263, 423, 961, 231, 993, 455, 801, 487, 721, 545, 295,
        529, 199, 625, 52, 163, 80, 20, 116,
    ),
    (
        545, 833, 769, 961, 929, 395, 875, 363, 993, 649, 907, 18,
        585, 801, 335, 753, 706, 271, 530, 431, 610, 681, 156, 463,
        54, 495, 86, 303, 114, 252, 216, 188,
    ),
)


def kernel(x_ref, wg_ref, wu_ref, wd_ref, out_ref, sum_ref,
           wg, wu, wd, xb, acc, hid, term, other, got, stage,
           w_sem, own_sem, load_sem,
           x_send, x_recv, d_send, d_recv, t_send, t_recv, s_send, s_recv):
    chunks = 8 * PARTS
    rows = xb.shape[1] // 2
    depth, cols = wg.shape
    wide = wd.shape[1]
    tile = 512

    dp = lax.axis_index("dp")
    tp = lax.axis_index("tp")
    core = lax.rem(tp, 2)
    chip = tp // 2
    y = chip // 4
    z = lax.rem(chip, 4)
    flip = z // 2
    outer = (z == 0) | (z == 3)
    away = 2 - 4 * flip
    mate = (dp, tp + 1 - 2 * core)
    peers = ((dp, tp + 8 - 16 * y), (dp, tp - away), (dp, tp + away))

    def pick(table, i):
        value = jnp.where(outer, table[0][0], table[1][0])
        for n in range(1, len(table[0])):
            value = jnp.where(i == n, jnp.where(outer, table[0][n], table[1][n]), value)
        return value

    def slot_of(chunk):
        source = chunk // PARTS
        sy = lax.rem(source // 4 + y, 2)
        sz = lax.rem(source, 4)
        sz = sz + flip * (3 - 2 * sz)
        return (sy * 4 + sz) * PARTS + lax.rem(chunk, PARTS)

    def bit(mask, n):
        return lax.rem(mask // (1 << n), 2) == 1

    loads = [
        pltpu.make_async_copy(src, dst, w_sem.at[n])
        for n, (src, dst) in enumerate(((wg_ref, wg), (wu_ref, wu), (wd_ref, wd)))
    ]
    mine = [
        pltpu.make_async_copy(
            x_ref.at[pl.ds(q * rows, rows)],
            xb.at[chip * PARTS + q, pl.ds(0, rows)],
            own_sem.at[q],
        )
        for q in range(PARTS)
    ]
    for copy in mine + loads:
        copy.start()

    barrier = pltpu.get_barrier_semaphore()
    for peer in (mate, peers[0], peers[2]):
        pl.semaphore_signal(barrier, inc=1, device_id=peer, device_id_type=MESH)

    @pl.when(jnp.logical_not(outer))
    def _():
        pl.semaphore_signal(barrier, inc=1, device_id=peers[1], device_id_type=MESH)

    pl.semaphore_wait(barrier, jnp.where(outer, 3, 4))

    def remote(src, dst, send, recv, peer):
        return pltpu.make_async_remote_copy(
            src_ref=src, dst_ref=dst, send_sem=send, recv_sem=recv,
            device_id=peer, device_id_type=MESH,
        )

    def rows_to(link, slot, src=None):
        here = xb.at[slot, pl.ds(0, rows)]
        return remote(
            here if src is None else src, here,
            x_send.at[link, slot], x_recv.at[slot], peers[link],
        )

    def share(slot, src=None):
        return remote(
            xb.at[slot, pl.ds(0, rows)] if src is None else src,
            xb.at[slot, pl.ds(rows, rows)],
            d_send.at[slot], d_recv.at[slot], mate,
        )

    def give(i):
        n = lax.rem(i, 2)
        return remote(term.at[n], other.at[n], t_send.at[n], t_recv.at[n], mate)

    def landing(slot, link):
        return sum_ref.at[slot * 3 + link]

    def fetch(slot, link):
        return pltpu.make_async_copy(landing(slot, link), got.at[link], load_sem.at[link])

    def sum_to(i, slot, link):
        n = lax.rem(i, STAGES)
        there = 0 if link == 0 else 2 if link == 1 else jnp.where(outer, 1, 2)
        return remote(
            stage.at[n], landing(slot, there), s_send.at[n], s_recv.at[slot * 3 + there],
            peers[link],
        )

    def keep(i, slot):
        n = lax.rem(i, STAGES)
        q = lax.rem(slot, PARTS)
        return pltpu.make_async_copy(
            stage.at[n], out_ref.at[pl.ds(pl.multiple_of(q * rows, rows), rows)], s_send.at[n]
        )

    def sent(i):
        n = lax.rem(i, STAGES)
        pltpu.make_async_copy(stage.at[n], stage.at[n], s_send.at[n]).wait()

    def pass_on(j, own=False):
        code = pick(PASS, j)
        chunk = code // 8
        mask = lax.rem(code, 8)
        slot = slot_of(chunk)
        src = None
        if own:
            q = lax.rem(chunk, PARTS)
            src = x_ref.at[pl.ds(pl.multiple_of(q * rows, rows), rows)]
        else:
            rows_to(0, slot).wait_recv()
        for link in (2, 1, 0):

            @pl.when(bit(mask, link))
            def _():
                rows_to(link, slot, src).start()

        share(slot, src).start()

    for j in range(PARTS):
        pass_on(j, own=True)
    for copy in mine + loads:
        copy.wait()

    @pl.loop(0, chunks + 1)
    def _(i):
        begin = jnp.where(i == 0, PARTS, pick(PASS_END, jnp.maximum(i - 1, 0)))
        end = pick(PASS_END, jnp.minimum(i, chunks - 1))

        def passing(j, carry):
            pass_on(j)
            return carry

        lax.fori_loop(begin, end, passing, 0)

        before = pick(WORK, jnp.maximum(i - 1, 0))
        slot_before = slot_of(before // 32)
        arriving = lax.rem(before // 4, 8)
        leaving = lax.rem(before, 4)

        @pl.when(i >= 1)
        def _():
            for link in range(3):

                @pl.when(bit(arriving, link))
                def _():
                    remote(
                        landing(slot_before, link), landing(slot_before, link),
                        s_send.at[0], s_recv.at[slot_before * 3 + link], mate,
                    ).wait_recv()
                    fetch(slot_before, link).start()

        @pl.when(i < chunks)
        def _():
            slot = slot_of(pick(WORK, jnp.minimum(i, chunks - 1)) // 32)
            share(slot).wait_recv()
            for n in range(cols // 256):
                part = pl.ds(n * 256, 256)
                gate = jnp.dot(xb[slot], wg[:, part], preferred_element_type=jnp.float32)
                up = jnp.dot(xb[slot], wu[:, part], preferred_element_type=jnp.float32)
                hid[:, part] = (jax.nn.silu(gate) * up).astype(hid.dtype)

        @pl.when(i >= 1)
        def _():
            for link in range(3):

                @pl.when(bit(arriving, link))
                def _():
                    fetch(slot_before, link).wait()
                    for n in range(wide // tile):
                        part = pl.ds(n * tile, tile)
                        acc[:, part] += got[link, :, part].astype(jnp.float32)

            give(i - 1).wait_recv()

            @pl.when(i - 1 >= STAGES)
            def _():
                sent(i - 1)

            for n in range(wide // tile):
                part = pl.ds(n * tile, tile)
                stage[lax.rem(i - 1, STAGES), :, part] = (
                    acc[:, part] + other[lax.rem(i - 1, 2), :, part].astype(jnp.float32)
                ).astype(stage.dtype)
            for link in range(3):

                @pl.when(leaving == 1 + link)
                def _():
                    sum_to(i - 1, slot_before, link).start()

            @pl.when(leaving == 0)
            def _():
                keep(i - 1, slot_before).start()

        @pl.when(i < chunks)
        def _():
            @pl.when(i >= 2)
            def _():
                give(i).wait_send()

            for n in range(wide // tile):
                part = pl.ds(n * tile, tile)
                both = jnp.dot(hid[...], wd[:, part], preferred_element_type=jnp.float32)
                acc[:, part] = both[:rows]
                term[lax.rem(i, 2), :, part] = both[rows:].astype(term.dtype)
            give(i).start()

    for i in range(2):
        give(i).wait_send()
    for i in range(STAGES):
        sent(i)

    @pl.loop(0, chunks)
    def _(j):
        code = pick(PASS, j)
        slot = slot_of(code // 8)
        for link in range(3):

            @pl.when(bit(lax.rem(code, 8), link))
            def _():
                rows_to(link, slot).wait_send()

        share(slot).wait_send()


def solution(mesh):
    def step(x, w_gate, w_up, w_down):
        total, depth = x.shape
        rows = total // PARTS
        chunks = 8 * PARTS
        cols = w_gate.shape[1]
        wide = w_down.shape[1]
        dma = pltpu.SemaphoreType.DMA
        b16, f32 = jnp.bfloat16, jnp.float32
        anywhere = pl.BlockSpec(memory_space=pl.ANY)
        out, _ = pl.pallas_call(
            kernel,
            name="ladder",
            out_shape=(
                jax.ShapeDtypeStruct((total, wide), b16),
                jax.ShapeDtypeStruct((chunks * 3, rows, wide), b16),
            ),
            in_specs=[anywhere] * 4,
            out_specs=(anywhere, anywhere),
            scratch_shapes=[
                pltpu.VMEM((depth, cols), b16),
                pltpu.VMEM((depth, cols), b16),
                pltpu.VMEM((cols, wide), b16),
                pltpu.VMEM((chunks, 2 * rows, depth), b16),
                pltpu.VMEM((rows, wide), f32),
                pltpu.VMEM((2 * rows, cols), b16),
                pltpu.VMEM((2, rows, wide), b16),
                pltpu.VMEM((2, rows, wide), b16),
                pltpu.VMEM((3, rows, wide), b16),
                pltpu.VMEM((STAGES, rows, wide), b16),
                dma((3,)), dma((PARTS,)), dma((3,)),
                dma((3, chunks)), dma((chunks,)), dma((chunks,)), dma((chunks,)),
                dma((2,)), dma((2,)), dma((STAGES,)), dma((chunks * 3,)),
            ],
            compiler_params=pltpu.CompilerParams(
                collective_id=0, has_side_effects=True, vmem_limit_bytes=67043328
            ),
            cost_estimate=pl.CostEstimate(
                flops=2 * 16 * total * depth * cols * 3,
                bytes_accessed=3 * depth * cols * 2 + 64 * total * depth * 2,
                transcendentals=16 * total * cols,
            ),
        )(x, w_gate, w_up, w_down)
        return out

    return jax.shard_map(
        step,
        mesh=mesh,
        in_specs=(P(("dp", "tp"), None), P(None, "tp"), P(None, "tp"), P("tp", None)),
        out_specs=P(("dp", "tp"), None),
        check_vma=False,
    )
```

time: 615 us -> 290 us (0.47)
  waiting for transfers between devices: 501 us -> 0 us
  Pallas kernels: 0 us -> 286 us
  matrix products: 99.9 us -> 0 us
  between operations: 13.4 us -> 0.01 us
    reduce_scatter x1 -> x0, waiting for transfers between devices: 328 us -> none  [step(): return lax.psum_scatter(term, 'tp', scatter_dimension=0, tiled=True)]
    pallas_call x0 -> x1, Pallas kernels: none -> 286 us  [step(): pl.pallas_call(kernel, name='ladder', out_shape=(jax.ShapeDtypeStruct((to...]
    all_gather x1 -> x0, waiting for transfers between devices: 172 us -> none  [step(): rows = lax.all_gather(x, 'tp', axis=0, tiled=True)]
    dot_general x3 -> x0, matrix products: 99.9 us -> none  [the longest x1 34.2 us: step(): jnp.dot(hidden, w_down, preferred_element_type=jnp.float32)]
  transfers between devices with their start and end apart: 2 -> 0, of which waited for: 2 -> 0; matrix products, arithmetic and copies ran while one was open for 0% -> 0% of each run, Pallas kernels for 0% -> 0%
where the time goes in v2:
time: 290 us; the launch traced here: 289 us
  Pallas kernels  286 us (99%)
  local copies, waits for them, and re-layouts  3.13 us (1%)
    pallas_call x1, Pallas kernels, step(): pl.pallas_call(kernel, name='ladder', out_shape=(jax.ShapeDtypeStruct((to...  286 us

profile of v2, /device:TPU:0, one launch (start us, length us, event | category | flops | bytes accessed | tf_op | source)
XLA Modules:
  0.0 289.5 jit_solution(14475302906553349305)
XLA Ops:
  0.0 286.3 %ladder.1 = (bf16[256,4096]{1,0:T(8,128)(2,1)}, bf16[96,64,4096]{2,1,0:T(8,128)(2,1)}) custom-call(bf16[256,4096]{1,0:T(8,128)(2,1)} %x_ref.1, bf16[4096,768]{1,0:T(8,128)(2,1)} %wg_ref.1, bf16[4096,768]{1,0:T(8,128)(2,1)} %wu_ref.1, bf16[768,4096]{1,0:T(8,128)(2,1)} %wd_ref.1), custom_call_target="tpu_custom_call" | custom-call | flops 77309411328 | bytes 153092096 | tf_op jit(solution)/shard_map/ladder/pallas_call | solution.py:298
  286.3 3.1 %copy.6 = bf16[256,4096]{1,0:T(8,128)(2,1)} copy(bf16[256,4096]{1,0:T(8,128)(2,1)} %get-tuple-element.6) | data formatting | bytes 4194304

commit v3 on v2

--- a/solution.py
+++ b/solution.py
@@ -12,38 +12,38 @@
 MESH = pl.DeviceIdType.MESH
 PASS = (
     (
-        5, 28, 13, 20, 57, 140, 49, 33, 89, 169, 160, 97,
-        209, 216, 193, 224, 184, 233, 80, 40, 144, 64, 176, 152,
-        104, 241, 248, 200, 112, 120, 72, 128,
-    ),
-    (
-        62, 51, 45, 39, 91, 5, 180, 65, 170, 160, 98, 140,
-        17, 29, 211, 194, 150, 234, 158, 80, 220, 132, 75, 243,
-        12, 250, 224, 202, 184, 122, 104, 112,
+        5, 28, 12, 21, 57, 41, 148, 49, 89, 132, 65, 220,
+        81, 113, 120, 192, 240, 168, 104, 225, 184, 248, 96, 232,
+        208, 200, 161, 72, 136, 32, 176, 152,
+    ),
+    (
+        63, 37, 47, 55, 90, 67, 28, 20, 0, 13, 82, 123,
+        115, 192, 132, 144, 180, 107, 227, 216, 240, 254, 234, 184,
+        75, 202, 162, 138, 154, 96, 168, 208,
     ),
 )
 PASS_END = (
     (
-        9, 11, 11, 13, 16, 16, 16, 16, 21, 21, 22, 23,
-        26, 26, 26, 26, 27, 29, 29, 30, 30, 31, 32, 32,
+        7, 11, 11, 13, 15, 16, 16, 20, 21, 22, 22, 24,
+        24, 24, 25, 25, 25, 27, 28, 28, 29, 31, 31, 31,
         32, 32, 32, 32, 32, 32, 32, 32,
     ),
     (
-        12, 16, 19, 24, 24, 25, 26, 27, 27, 29, 29, 29,
-        29, 29, 29, 31, 31, 31, 31, 31, 32, 32, 32, 32,
+        15, 16, 20, 21, 25, 25, 25, 25, 26, 27, 27, 27,
+        27, 28, 31, 31, 31, 31, 31, 31, 31, 32, 32, 32,
         32, 32, 32, 32, 32, 32, 32, 32,
     ),
 )
 WORK = (
     (
-        131, 355, 643, 387, 867, 675, 833, 899, 769, 929, 579, 327,
-        737, 263, 423, 961, 231, 993, 455, 801, 487, 721, 545, 295,
-        529, 199, 625, 52, 163, 80, 20, 116,
-    ),
-    (
-        545, 833, 769, 961, 929, 395, 875, 363, 993, 649, 907, 18,
-        585, 801, 335, 753, 706, 271, 530, 431, 610, 681, 156, 463,
-        54, 495, 86, 303, 114, 252, 216, 188,
+        579, 161, 355, 867, 451, 481, 771, 963, 417, 897, 999, 321,
+        679, 737, 935, 391, 259, 817, 641, 839, 513, 295, 705, 135,
+        231, 625, 561, 199, 80, 100, 20, 36,
+    ),
+    (
+        35, 587, 707, 899, 97, 875, 363, 481, 433, 802, 777, 985,
+        641, 1007, 529, 753, 681, 943, 463, 395, 630, 562, 271, 857,
+        82, 299, 22, 327, 156, 252, 180, 216,
     ),
 )
 

time: 290 us -> 274 us (0.945)
  Pallas kernels: 286 us -> 270 us
    pallas_call x1, Pallas kernels: 286 us -> 270 us  [step(): pl.pallas_call(kernel, name='ladder', out_shape=(jax.ShapeDtypeStruct((to...]
where the time goes in v3:
time: 274 us
  Pallas kernels  270 us (99%)
  local copies, waits for them, and re-layouts  3.13 us (1%)
    pallas_call x1, Pallas kernels, step(): pl.pallas_call(kernel, name='ladder', out_shape=(jax.ShapeDtypeStruct((to...  270 us

profile of v3, /device:TPU:0, one launch (start us, length us, event | category | flops | bytes accessed | tf_op | source)
XLA Modules:
  0.0 273.6 jit_solution(6577880888442641292)
XLA Ops:
  0.0 270.5 %ladder.1 = (bf16[256,4096]{1,0:T(8,128)(2,1)}, bf16[96,64,4096]{2,1,0:T(8,128)(2,1)}) custom-call(bf16[256,4096]{1,0:T(8,128)(2,1)} %x_ref.1, bf16[4096,768]{1,0:T(8,128)(2,1)} %wg_ref.1, bf16[4096,768]{1,0:T(8,128)(2,1)} %wu_ref.1, bf16[768,4096]{1,0:T(8,128)(2,1)} %wd_ref.1), custom_call_target="tpu_custom_call" | custom-call | flops 77309411328 | bytes 153092096 | tf_op jit(solution)/shard_map/ladder/pallas_call | solution.py:298
  270.5 3.1 %copy.6 = bf16[256,4096]{1,0:T(8,128)(2,1)} copy(bf16[256,4096]{1,0:T(8,128)(2,1)} %get-tuple-element.6) | data formatting | bytes 4194304

commit v4 on v3

v4 whole, which is shorter than its diff:
```python
import functools

import jax
import jax.numpy as jnp
from jax import lax
from jax.experimental import pallas as pl
from jax.experimental.pallas import tpu as pltpu
from jax.sharding import PartitionSpec as P

PARTS = 4
STAGES = 16
MESH = pl.DeviceIdType.MESH
PASS = (
    (
        53, 28, 37, 61, 1, 21, 9, 45, 292, 260, 105, 268,
        65, 276, 329, 300, 97, 364, 81, 249, 320, 72, 352, 241,
        176, 336, 153, 504, 217, 496, 408, 209, 185, 489, 481, 401,
        112, 472, 432, 464, 304, 448, 376, 424, 440, 456, 392, 192,
        232, 224, 384, 416, 200, 128, 144, 136, 368, 312, 120, 168,
        160, 345, 280, 88,
    ),
    (
        127, 92, 77, 87, 119, 106, 99, 67, 61, 334, 155, 53,
        29, 292, 179, 340, 250, 20, 243, 378, 261, 324, 187, 219,
        32, 300, 434, 144, 210, 316, 364, 356, 269, 44, 490, 483,
        402, 451, 394, 504, 387, 412, 427, 459, 276, 224, 419, 194,
        496, 440, 130, 8, 202, 232, 138, 370, 170, 464, 304, 162,
        472, 346, 282, 0,
    ),
)
PASS_END = (
    (
        18, 22, 26, 27, 28, 33, 33, 35, 38, 39, 43, 43,
        46, 49, 52, 53, 53, 57, 57, 58, 58, 61, 62, 62,
        63, 63, 63, 64, 64, 64, 64, 64,
    ),
    (
        23, 33, 34, 40, 42, 50, 50, 52, 52, 52, 52, 60,
        62, 62, 63, 63, 63, 63, 63, 63, 63, 64, 64, 64,
        64, 64, 64, 64, 64, 64, 64, 64,
    ),
)
WORK = (
    (
        6243, 20579, 15395, 22627, 18465, 13347, 11363, 30753, 31971, 4195, 29923, 25697,
        28705, 27747, 24609, 14567, 26657, 12519, 8423, 23585, 16417, 10471, 9319, 21537,
        7399, 17969, 20017, 5351, 2708, 1156, 660, 3732,
    ),
    (
        1121, 16483, 15401, 30755, 13865, 24611, 11563, 29233, 32239, 18481, 22825, 3138,
        26657, 30191, 20793, 25891, 28139, 18006, 14827, 20050, 12783, 24113, 21553, 8683,
        2774, 10735, 594, 9707, 5020, 7580, 7068, 6044,
    ),
)


def kernel(x_ref, wg_ref, wu_ref, wd_ref, out_ref, sum_ref,
           wg, wu, wd, xb, acc, hid, term, other, got, stage,
           w_sem, own_sem, load_sem,
           x_send, x_recv, d_send, d_recv, t_send, t_recv, s_send, s_recv):
    chunks = 8 * PARTS
    rows = xb.shape[1] // 2
    half = rows // 2
    depth, cols = wg.shape
    wide = wd.shape[1]
    tile = 512

    dp = lax.axis_index("dp")
    tp = lax.axis_index("tp")
    core = lax.rem(tp, 2)
    chip = tp // 2
    y = chip // 4
    z = lax.rem(chip, 4)
    flip = z // 2
    outer = (z == 0) | (z == 3)
    away = 2 - 4 * flip
    mate = (dp, tp + 1 - 2 * core)
    peers = ((dp, tp + 8 - 16 * y), (dp, tp - away), (dp, tp + away))

    def pick(table, i):
        value = jnp.where(outer, table[0][0], table[1][0])
        for n in range(1, len(table[0])):
            value = jnp.where(i == n, jnp.where(outer, table[0][n], table[1][n]), value)
        return value

    def slot_of(chunk):
        source = chunk // PARTS
        sy = lax.rem(source // 4 + y, 2)
        sz = lax.rem(source, 4)
        sz = sz + flip * (3 - 2 * sz)
        return (sy * 4 + sz) * PARTS + lax.rem(chunk, PARTS)

    def bit(mask, n):
        return lax.rem(mask // (1 << n), 2) == 1

    loads = [
        pltpu.make_async_copy(src, dst, w_sem.at[n])
        for n, (src, dst) in enumerate(((wg_ref, wg), (wu_ref, wu), (wd_ref, wd)))
    ]
    mine = [
        pltpu.make_async_copy(
            x_ref.at[pl.ds(q * rows, rows)],
            xb.at[chip * PARTS + q, pl.ds(0, rows)],
            own_sem.at[q],
        )
        for q in range(PARTS)
    ]
    for copy in mine + loads:
        copy.start()

    barrier = pltpu.get_barrier_semaphore()
    for peer in (mate, peers[0], peers[2]):
        pl.semaphore_signal(barrier, inc=1, device_id=peer, device_id_type=MESH)

    @pl.when(jnp.logical_not(outer))
    def _():
        pl.semaphore_signal(barrier, inc=1, device_id=peers[1], device_id_type=MESH)

    pl.semaphore_wait(barrier, jnp.where(outer, 3, 4))

    def remote(src, dst, send, recv, peer):
        return pltpu.make_async_remote_copy(
            src_ref=src, dst_ref=dst, send_sem=send, recv_sem=recv,
            device_id=peer, device_id_type=MESH,
        )

    def piece_at(core_rows, piece):
        start = core_rows * rows + lax.rem(piece, 2) * half
        return xb.at[piece // 2, pl.ds(pl.multiple_of(start, half), half)]

    def rows_to(link, piece, j=0, src=None):
        here = piece_at(0, piece)
        return remote(
            here if src is None else src, here,
            x_send.at[link, j], x_recv.at[piece], peers[link],
        )

    def share(piece, j=0, src=None):
        return remote(
            piece_at(0, piece) if src is None else src, piece_at(1, piece),
            d_send.at[j], d_recv.at[piece], mate,
        )

    def give(i):
        n = lax.rem(i, 2)
        return remote(term.at[n], other.at[n], t_send.at[n], t_recv.at[n], mate)

    def landing(piece, link):
        return sum_ref.at[piece * 3 + link]

    def fetch(piece, h, link):
        return pltpu.make_async_copy(
            landing(piece, link), got.at[link, pl.ds(h * half, half)], load_sem.at[link, h]
        )

    def staged(i, h):
        return stage.at[lax.rem(i, STAGES), pl.ds(h * half, half)]

    def sum_to(i, h, piece, link):
        there = 0 if link == 0 else 2 if link == 1 else jnp.where(outer, 1, 2)
        return remote(
            staged(i, h), landing(piece, there), s_send.at[lax.rem(i, STAGES), h],
            s_recv.at[piece * 3 + there], peers[link],
        )

    def keep(i, h, piece):
        start = lax.rem(piece, 2 * PARTS) * half
        return pltpu.make_async_copy(
            staged(i, h), out_ref.at[pl.ds(pl.multiple_of(start, half), half)],
            s_send.at[lax.rem(i, STAGES), h],
        )

    def sent(i):
        for h in range(2):
            pltpu.make_async_copy(
                staged(i, h), staged(i, h), s_send.at[lax.rem(i, STAGES), h]
            ).wait()

    def piece_of(code):
        name = code // 8
        return slot_of(name // 2) * 2 + lax.rem(name, 2)

    def pass_on(j, own=False):
        code = pick(PASS, j)
        mask = lax.rem(code, 8)
        piece = piece_of(code)
        src = None
        if own:
            start = lax.rem(piece, 2 * PARTS) * half
            src = x_ref.at[pl.ds(pl.multiple_of(start, half), half)]
        else:
            rows_to(0, piece).wait_recv()
        for link in (2, 1, 0):

            @pl.when(bit(mask, link))
            def _():
                rows_to(link, piece, j, src).start()

        share(piece, j, src).start()

    for j in range(2 * PARTS):
        pass_on(j, own=True)
    for copy in mine + loads:
        copy.wait()

    @pl.loop(0, chunks + 1)
    def _(i):
        begin = jnp.where(i == 0, 2 * PARTS, pick(PASS_END, jnp.maximum(i - 1, 0)))
        end = pick(PASS_END, jnp.minimum(i, chunks - 1))

        def passing(j, carry):
            pass_on(j)
            return carry

        lax.fori_loop(begin, end, passing, 0)

        before = pick(WORK, jnp.maximum(i - 1, 0))
        slot_before = slot_of(before // 1024)
        halves = (lax.rem(before, 32), lax.rem(before // 32, 32))

        @pl.when(i >= 1)
        def _():
            for h in range(2):
                piece = slot_before * 2 + h
                for link in range(3):

                    @pl.when(bit(halves[h] // 4, link))
                    def _():
                        remote(
                            landing(piece, link), landing(piece, link),
                            s_send.at[0, 0], s_recv.at[piece * 3 + link], mate,
                        ).wait_recv()
                        fetch(piece, h, link).start()

        @pl.when(i < chunks)
        def _():
            slot = slot_of(pick(WORK, jnp.minimum(i, chunks - 1)) // 1024)
            for h in range(2):
                share(slot * 2 + h).wait_recv()
            for n in range(cols // 256):
                part = pl.ds(n * 256, 256)
                gate = jnp.dot(xb[slot], wg[:, part], preferred_element_type=jnp.float32)
                up = jnp.dot(xb[slot], wu[:, part], preferred_element_type=jnp.float32)
                hid[:, part] = (jax.nn.silu(gate) * up).astype(hid.dtype)

        @pl.when(i >= 1)
        def _():
            for h in range(2):
                for link in range(3):

                    @pl.when(bit(halves[h] // 4, link))
                    def _():
                        fetch(slot_before * 2 + h, h, link).wait()
                        for n in range(wide // tile):
                            at = (pl.ds(h * half, half), pl.ds(n * tile, tile))
                            acc[at] += got[(link, *at)].astype(jnp.float32)

            give(i - 1).wait_recv()

            @pl.when(i - 1 >= STAGES)
            def _():
                sent(i - 1)

            for n in range(wide // tile):
                part = pl.ds(n * tile, tile)
                stage[lax.rem(i - 1, STAGES), :, part] = (
                    acc[:, part] + other[lax.rem(i - 1, 2), :, part].astype(jnp.float32)
                ).astype(stage.dtype)
            for h in range(2):
                piece = slot_before * 2 + h
                leaving = lax.rem(halves[h], 4)
                for link in range(3):

                    @pl.when(leaving == 1 + link)
                    def _():
                        sum_to(i - 1, h, piece, link).start()

                @pl.when(leaving == 0)
                def _():
                    keep(i - 1, h, piece).start()

        @pl.when(i < chunks)
        def _():
            @pl.when(i >= 2)
            def _():
                give(i).wait_send()

            for n in range(wide // tile):
                part = pl.ds(n * tile, tile)
                both = jnp.dot(hid[...], wd[:, part], preferred_element_type=jnp.float32)
                acc[:, part] = both[:rows]
                term[lax.rem(i, 2), :, part] = both[rows:].astype(term.dtype)
            give(i).start()

    for i in range(2):
        give(i).wait_send()
    for i in range(STAGES):
        sent(i)

    for kind, here in enumerate((outer, jnp.logical_not(outer))):

        @pl.when(here)
        def _():
            for j, code in enumerate(PASS[kind]):
                for link in range(3):
                    if code >> link & 1:
                        rows_to(link, 0, j).wait_send()
                share(0, j).wait_send()


def solution(mesh):
    def step(x, w_gate, w_up, w_down):
        total, depth = x.shape
        rows = total // PARTS
        chunks = 8 * PARTS
        cols = w_gate.shape[1]
        wide = w_down.shape[1]
        dma = pltpu.SemaphoreType.DMA
        b16, f32 = jnp.bfloat16, jnp.float32
        anywhere = pl.BlockSpec(memory_space=pl.ANY)
        out, _ = pl.pallas_call(
            kernel,
            name="ladder",
            out_shape=(
                jax.ShapeDtypeStruct((total, wide), b16),
                jax.ShapeDtypeStruct((chunks * 6, rows // 2, wide), b16),
            ),
            in_specs=[anywhere] * 4,
            out_specs=(anywhere, anywhere),
            scratch_shapes=[
                pltpu.VMEM((depth, cols), b16),
                pltpu.VMEM((depth, cols), b16),
                pltpu.VMEM((cols, wide), b16),
                pltpu.VMEM((chunks, 2 * rows, depth), b16),
                pltpu.VMEM((rows, wide), f32),
                pltpu.VMEM((2 * rows, cols), b16),
                pltpu.VMEM((2, rows, wide), b16),
                pltpu.VMEM((2, rows, wide), b16),
                pltpu.VMEM((3, rows, wide), b16),
                pltpu.VMEM((STAGES, rows, wide), b16),
                dma((3,)), dma((PARTS,)), dma((3, 2)),
                dma((3, 2 * chunks)), dma((2 * chunks,)), dma((2 * chunks,)), dma((2 * chunks,)),
                dma((2,)), dma((2,)), dma((STAGES, 2)), dma((chunks * 6,)),
            ],
            compiler_params=pltpu.CompilerParams(
                collective_id=0, has_side_effects=True, vmem_limit_bytes=67043328
            ),
            cost_estimate=pl.CostEstimate(
                flops=2 * 16 * total * depth * cols * 3,
                bytes_accessed=3 * depth * cols * 2 + 64 * total * depth * 2,
                transcendentals=16 * total * cols,
            ),
        )(x, w_gate, w_up, w_down)
        return out

    return jax.shard_map(
        step,
        mesh=mesh,
        in_specs=(P(("dp", "tp"), None), P(None, "tp"), P(None, "tp"), P("tp", None)),
        out_specs=P(("dp", "tp"), None),
        check_vma=False,
    )
```

time: 274 us -> 269 us (0.982)
  Pallas kernels: 270 us -> 266 us
    pallas_call x1, Pallas kernels: 270 us -> 266 us  [step(): pl.pallas_call(kernel, name='ladder', out_shape=(jax.ShapeDtypeStruct((to...]
where the time goes in v4:
time: 269 us
  Pallas kernels  266 us (99%)
  local copies, waits for them, and re-layouts  3.13 us (1%)
    pallas_call x1, Pallas kernels, step(): pl.pallas_call(kernel, name='ladder', out_shape=(jax.ShapeDtypeStruct((to...  266 us

profile of v4, /device:TPU:0, one launch (start us, length us, event | category | flops | bytes accessed | tf_op | source)
XLA Modules:
  0.0 268.7 jit_solution(16327229216425004329)
XLA Ops:
  0.0 265.5 %ladder.1 = (bf16[256,4096]{1,0:T(8,128)(2,1)}, bf16[192,32,4096]{2,1,0:T(8,128)(2,1)}) custom-call(bf16[256,4096]{1,0:T(8,128)(2,1)} %x_ref.1, bf16[4096,768]{1,0:T(8,128)(2,1)} %wg_ref.1, bf16[4096,768]{1,0:T(8,128)(2,1)} %wu_ref.1, bf16[768,4096]{1,0:T(8,128)(2,1)} %wd_ref.1), custom_call_target="tpu_custom_call" | custom-call | flops 77309411328 | bytes 153092096 | tf_op jit(solution)/shard_map/ladder/pallas_call | solution.py:321
  265.5 3.1 %copy.6 = bf16[256,4096]{1,0:T(8,128)(2,1)} copy(bf16[256,4096]{1,0:T(8,128)(2,1)} %get-tuple-element.6) | data formatting | bytes 4194304
